TPU v7x, 8 devices: a whole 2x2x1 slice. The times are simulated.
8 devices in a mesh: dp: 1 (over z), rep: 2 (over y), team: 4 (over x, core).
Axes of the slice: x: 2, y: 2, z: 1, core: 2. Of those that a mesh axis runs over, the one named last changes fastest.
Arguments:
- points: bfloat16 [8192, 90], P(('dp', 'team', 'rep'))
- values: bfloat16 [8192, 1], P(('dp', 'team', 'rep'))
- pair_mask: int32 [4, 4], P('dp')
- bandwidth: float32 [1], replicated
Outputs:
- output: float32 [8192, 1], P(('dp', 'team', 'rep'))
All inputs are finite; a program needn't handle non-finite values.
Results may differ from a plain program's by a relative error of at most 0.00585081.
Values are sent between devices in bfloat16 or wider.
A program may use at most 1 GiB of HBM per device.

v0:
```python
import jax
import jax.numpy as jnp
from jax import lax
from jax.sharding import PartitionSpec as P


def solution(mesh):
    rep_n = mesh.shape["rep"]
    team_n = mesh.shape["team"]
    layer_span = team_n // rep_n
    row_spec = P(("dp", "team", "rep"), None)
    first_perm = [(layer_id * team_n + source, layer_id * team_n + (source - layer_id * layer_span) % team_n) for layer_id in range(rep_n) for source in range(team_n)]
    shift_perm = [(source, (source - 1) % team_n) for source in range(team_n)]

    def per_device(points_dev, values_dev, pair_mask, bandwidth):
        width = bandwidth[0]
        home_pts = lax.all_gather(points_dev, "rep", axis=0, tiled=True)
        home_vals = lax.all_gather(values_dev, "rep", axis=0, tiled=True)
        home_sq = jnp.sum(jnp.square(home_pts.astype(jnp.float32)), axis=1)
        team_idx = lax.axis_index("team")
        rep_idx = lax.axis_index("rep")
        mask_row = lax.dynamic_index_in_dim(pair_mask, team_idx, axis=0, keepdims=False).astype(jnp.float32)
        start_block = (team_idx + rep_idx * layer_span) % team_n

        def block_term(vis_pts, vis_vals, key_block):
            vis_sq = jnp.sum(jnp.square(vis_pts.astype(jnp.float32)), axis=1)
            cross_dot = jnp.einsum("id,jd->ij", home_pts, vis_pts, preferred_element_type=jnp.float32)
            sq_dist = home_sq[:, None] + vis_sq[None, :] - 2.0 * cross_dot
            kernel = jnp.exp(-sq_dist / width).astype(jnp.bfloat16)
            contrib = jnp.dot(kernel, vis_vals, preferred_element_type=jnp.float32)
            return mask_row[key_block] * contrib

        first_pts = lax.ppermute(home_pts, ("rep", "team"), first_perm)
        first_vals = lax.ppermute(home_vals, ("rep", "team"), first_perm)
        row_sum = block_term(first_pts, first_vals, start_block)

        def shift_step(step_idx, state):
            total, cur_pts, cur_vals = state
            cur_pts = lax.ppermute(cur_pts, "team", shift_perm)
            cur_vals = lax.ppermute(cur_vals, "team", shift_perm)
            key_block = (start_block + step_idx) % team_n
            return (total + block_term(cur_pts, cur_vals, key_block), cur_pts, cur_vals)

        row_sum, _, _ = lax.fori_loop(1, layer_span, shift_step, (row_sum, first_pts, first_vals))
        return lax.psum_scatter(row_sum, "rep", scatter_dimension=0, tiled=True)

    return jax.shard_map(per_device, mesh=mesh, in_specs=(row_spec, row_spec, P("dp", None), P()), out_specs=row_spec, check_vma=False)
```

profile of v0, /device:TPU:0, one launch (start us, length us, event | category | flops | bytes accessed | tf_op | source)
XLA Modules:
  0.0 71.3 jit_solution(5619286285482382990)
XLA Ops:
  6.5 0.0 reduce-scatter.4.cloned.1.call-start
  6.5 8.9 %all_gather.6 = bf16[2048,90]{0,1:T(8,128)(2,1)S(1)} all-gather(bf16[1024,90]{0,1:T(8,128)(2,1)} %param.4), channel_id=1, replica_groups=mesh['dp'=1,'rep'=2,'team'=4] {'rep'}, dimensions={0}, use_global_device_ids=true | all-gather | bytes 552960 | tf_op jit(solution)/shard_map/all_gather | solution.py:17
  15.4 0.7 collective-permute-start
  16.1 6.8 %all_gather.7 = bf16[2048,1]{0,1:T(2,128)(2,1)S(1)} all-gather(bf16[1024,1]{0,1:T(2,128)(2,1)} %param.5), channel_id=1, replica_groups=mesh['dp'=1,'rep'=2,'team'=4] {'rep'}, dimensions={0}, use_global_device_ids=true | all-gather | bytes 6144 | tf_op jit(solution)/shard_map/all_gather | solution.py:18
  22.9 0.7 collective-permute-start.1
  23.6 0.1 multiply_reduce_fusion.2
  23.7 0.7 fusion.2
  25.0 0.7 constant_dynamic-slice_fusion.1
  25.7 0.0 collective-permute-done.1
  25.7 0.0 collective-permute-start.3
  25.7 0.0 collective-permute-done
  25.7 0.1 multiply_reduce_fusion.1
  25.8 0.7 collective-permute-start.2
  26.5 5.7 %fusion = f32[1,2048]{1,0:T(1,128)S(1)} fusion(bf16[2048,1]{0,1:T(2,128)(2,1)S(1)} %collective-permute-done.1, bf16[2048,90]{0,1:T(8,128)(2,1)S(1)} %all_gather.6, bf16[2048,90]{0,1:T(8,128)(2,1)S(1)} %collective-permute-done, f32[]{:T(128)} %bitcast.13, f32[2048]{0:T(1024)S(1)} %multiply_reduce_fusion.1, f32[2048]{0:T(1024)S(1)} %multiply_reduce_fusion.2), kind=kOutput, calls=%fused_computation.2 | convolution fusion | flops 788529152 | bytes 765956 | tf_op jit(solution)/shard_map/dot_general | solution.py:30
  32.2 0.0 collective-permute-done.2
  32.2 0.1 multiply_reduce_fusion
  32.3 0.0 collective-permute-done.3
  32.3 5.7 %fusion.1 = f32[1,2048]{1,0:T(1,128)S(1)} fusion(bf16[2048,1]{0,1:T(2,128)(2,1)S(1)} %collective-permute-done.3, bf16[2048,90]{0,1:T(8,128)(2,1)S(1)} %all_gather.6, bf16[2048,90]{0,1:T(8,128)(2,1)S(1)} %collective-permute-done.2, f32[2048]{0:T(1024)S(1)} %multiply_reduce_fusion, f32[]{:T(128)} %bitcast.14, f32[2048]{0:T(1024)S(1)} %multiply_reduce_fusion.2), kind=kOutput, calls=%fused_computation.3 | convolution fusion | flops 788529152 | bytes 765956 | tf_op jit(solution)/shard_map/while/body/eval_jaxpr/dot_general | solution.py:30
  38.0 1.3 %multiply_add_fusion = f32[2048]{0:T(1024)S(1)} fusion(f32[2048]{0:T(1024)S(1)} %bitcast.17, f32[2048]{0:T(1024)S(1)} %bitcast.16, f32[]{:T(128)} %bitcast.3, f32[]{:T(128)} %bitcast), kind=kLoop, calls=%fused_computation.7 | loop fusion | flops 6144 | bytes 24584 | tf_op jit(solution)/shard_map/while/body/eval_jaxpr/add | solution.py:42
  39.3 1.4 %copy.5 = f32[2048,1]{1,0:T(8,128)} copy(f32[2048,1]{0,1:T(1,128)S(1)} %bitcast.15) | data formatting | bytes 16384
  40.7 0.0 reduce-scatter.4.cloned.1.call-update
  40.7 22.0 %reduce-scatter.4.cloned.1.call-done = f32[1024,1]{1,0:T(8,128)} async-done(((f32[2048,1]{1,0:T(8,128)}), f32[1024,1]{1,0:T(8,128)}) %reduce-scatter.4.cloned.1.call-update) | async-done | bytes 4112
  62.7 1.8 %copy.6 = f32[1024,1]{0,1:T(1,128)} copy(f32[1024,1]{1,0:T(8,128)} %reduce-scatter.4.cloned.1.call-done) | data formatting | bytes 8192
Async XLA Ops:
  6.5 56.1 %reduce-scatter.4.cloned.1.call-start = ((), (), s32[]{:S(2)}) async-start(), calls=%async_computation.1 | async-start | bytes 1572864
  15.4 10.3 %collective-permute-start = (bf16[2048,90]{0,1:T(8,128)(2,1)S(1)}, bf16[2048,90]{0,1:T(8,128)(2,1)S(1)}, u32[]{:S(2)}, u32[]{:S(2)}) collective-permute-start(bf16[2048,90]{0,1:T(8,128)(2,1)S(1)} %all_gather.6), channel_id=1, source_target_pairs={{0,0},{1,1},{2,2},{3,3},{4,6},{5,7},{6,4},{7,5}} | collective-permute-start | bytes 1105928 | tf_op jit(solution)/shard_map/ppermute | solution.py:33
  22.9 2.8 %collective-permute-start.1 = (bf16[2048,1]{0,1:T(2,128)(2,1)S(1)}, bf16[2048,1]{0,1:T(2,128)(2,1)S(1)}, u32[]{:S(2)}, u32[]{:S(2)}) collective-permute-start(bf16[2048,1]{0,1:T(2,128)(2,1)S(1)} %all_gather.7), channel_id=1, source_target_pairs={{0,0},{1,1},{2,2},{3,3},{4,6},{5,7},{6,4},{7,5}} | collective-permute-start | bytes 12296 | tf_op jit(solution)/shard_map/ppermute | solution.py:34
  25.7 6.6 %collective-permute-start.3 = (bf16[2048,1]{0,1:T(2,128)(2,1)S(1)}, bf16[2048,1]{0,1:T(2,128)(2,1)S(1)}, u32[]{:S(2)}, u32[]{:S(2)}) collective-permute-start(bf16[2048,1]{0,1:T(2,128)(2,1)S(1)} %collective-permute-done.1), channel_id=1, source_target_pairs={{0,3},{1,0},{2,1},{3,2},{4,7},{5,4},{6,5},{7,6}} | collective-permute-start | bytes 12296 | tf_op jit(solution)/shard_map/while/body/eval_jaxpr/ppermute | solution.py:40
  25.8 6.4 %collective-permute-start.2 = (bf16[2048,90]{0,1:T(8,128)(2,1)S(1)}, bf16[2048,90]{0,1:T(8,128)(2,1)S(1)}, u32[]{:S(2)}, u32[]{:S(2)}) collective-permute-start(bf16[2048,90]{0,1:T(8,128)(2,1)S(1)} %collective-permute-done), channel_id=1, source_target_pairs={{0,3},{1,0},{2,1},{3,2},{4,7},{5,4},{6,5},{7,6}} | collective-permute-start | bytes 1105928 | tf_op jit(solution)/shard_map/while/body/eval_jaxpr/ppermute | solution.py:39
Sparse Core Ops, SparseCore 0:
  40.8 21.7 reduce-scatter.3
where the time goes:
time: 71.6 us; the launch traced here: 71.3 us
  waiting for transfers between devices  22 us (31%)
  blocking collectives  15.7 us (22%)
  between operations  14.1 us (20%)
  matrix products  11.4 us (16%)
  local copies, waits for them, and re-layouts  3.85 us (5%)
  other arithmetic  2.27 us (3%)
  starting transfers between devices  1.99 us (3%)
    unnamed x2, waiting for transfers between devices  22 us
    dot_general x2, matrix products, block_term(): contrib = jnp.dot(kernel, vis_vals, preferred_element_type=jnp.float32)  11.4 us
    all_gather x1, blocking collectives, per_device(): home_pts = lax.all_gather(points_dev, 'rep', axis=0, tiled=True)  8.91 us
    all_gather x1, blocking collectives, per_device(): home_vals = lax.all_gather(values_dev, 'rep', axis=0, tiled=True)  6.77 us
    unnamed x2, local copies, waits for them, and re-layouts  3.19 us
  transfers between devices with their start and end apart: 5, of which 1 were waited for; matrix products, arithmetic and copies ran while one was open for 10% of the time, Pallas kernels for 0%

commit v1 on v0

v1 whole, which is shorter than its diff:
```python
import functools

import jax
import jax.numpy as jnp
from jax import lax
from jax.experimental import pallas as pl
from jax.experimental.pallas import tpu as pltpu
from jax.sharding import PartitionSpec as P

MESH = pl.DeviceIdType.MESH
N = 1024
SUB = 256
LOG2E = 1.4426950408889634


def chunks(sizes):
    out, at = [], 0
    for size in sizes:
        out.append((at, size))
        at += size
    return out


C1 = chunks((512, 512))
C3 = chunks((512, 256, 256))
NK = 4


def split3(s):
    hi = s.astype(jnp.bfloat16).astype(jnp.float32)
    rest = s - hi
    mid = rest.astype(jnp.bfloat16).astype(jnp.float32)
    return hi, mid, rest - mid


def augment(xt, weights):
    n = xt.shape[1]
    x32 = xt.astype(jnp.float32)
    hi, mid, lo = split3(jnp.sum(x32 * x32, axis=0, keepdims=True))
    last = jnp.concatenate([x32[80:90], jnp.zeros((6, n), jnp.float32)], axis=0)
    row = lax.broadcasted_iota(jnp.int32, (16, n), 0)
    if weights:
        tail = jnp.where(row < 10, -2.0 * last, jnp.where(row < 13, 1.0, jnp.where(row == 13, hi, jnp.where(row == 14, mid, lo))))
        return jnp.concatenate([(-2.0 * x32[:80]).astype(jnp.bfloat16), tail.astype(jnp.bfloat16)], axis=0)
    tail = jnp.where(row < 10, last, jnp.where(row >= 13, 1.0, jnp.where(row == 10, hi, jnp.where(row == 11, mid, lo))))
    return jnp.concatenate([xt[:80], tail.astype(jnp.bfloat16)], axis=0)


def kernel(x_hbm, v_hbm, m_hbm, h_ref, o_ref, xb, vb, mb, wb, lb, fb, load_sem, send_sem, recv_sem, vsend_sem, vrecv_sem):
    y, t, dp = lax.axis_index("rep"), lax.axis_index("team"), lax.axis_index("dp")
    x, c = t // 2, t % 2

    def dev(dx, dy, dc):
        return (dp, y + dy - 2 * y * dy, 2 * (x + dx - 2 * x * dx) + c + dc - 2 * c * dc)

    partner, target, source, across = dev(0, 0, 1), dev(1 - c, c, 1), dev(c, 1 - c, 1), dev(1, 0, 0)
    third = dev(1 - c, c, c)

    bar = pltpu.get_barrier_semaphore()
    for d in (partner, source, across):
        pl.semaphore_signal(bar, inc=1, device_id=d, device_id_type=MESH)
    loads = [pltpu.make_async_copy(src, dst, load_sem.at[i]) for i, (src, dst) in enumerate(((x_hbm, xb.at[0]), (v_hbm, vb.at[0]), (m_hbm, mb)))]
    for z in loads:
        z.start()
    wb[96:256, :] = jnp.zeros((160, N), jnp.bfloat16)
    lb[...] = jnp.zeros_like(lb)

    sends = []

    def remote(src, dst, ssem, rsem, d):
        return pltpu.make_async_remote_copy(src_ref=src, dst_ref=dst, send_sem=ssem, recv_sem=rsem, device_id=d, device_id_type=MESH)

    def send_x(src, slot, at, k, lane, d):
        cols = pl.ds(at[0], at[1])
        z = remote(src.at[:, cols], xb.at[slot, :, cols], send_sem.at[lane, k], recv_sem.at[slot, k], d)
        z.start()
        return z

    def send_v(src, slot, lane, d):
        z = remote(src, vb.at[slot], vsend_sem.at[lane], vrecv_sem.at[slot], d)
        z.start()
        return z

    def recv_x(slot, at, k):
        ref = xb.at[slot, :, pl.ds(at[0], at[1])]
        remote(ref, ref, send_sem.at[0, k], recv_sem.at[slot, k], partner).wait_recv()

    def recv_v(slot):
        remote(vb.at[slot], vb.at[slot], vsend_sem.at[0], vrecv_sem.at[slot], partner).wait_recv()

    def compute(accs):
        fb[...] = jnp.zeros_like(fb)
        pl.semaphore_wait(bar, 3)
        sends.append(send_v(v_hbm, 5 + c, 0, target))
        for k, at in enumerate(C1):
            sends.append(send_x(x_hbm, 5 + c, at, k, 0, target))
        sends.append(send_v(v_hbm, 4, 1, partner))
        for k, at in enumerate(C1):
            sends.append(send_x(x_hbm, 4, at, k, 1, partner))
        loads[0].wait()
        loads[1].wait()
        alpha = -LOG2E / h_ref[0]
        for i in range(0, N, SUB):
            wb[0:96, i:i + SUB] = augment(xb[0, :, i:i + SUB], True)

        state = dict(ring=0, buf=0, pend=[])
        rows = lax.broadcasted_iota(jnp.int32, (16, SUB), 0)

        def flush(keep=0):
            pass

        def tiles(slot, team, at):
            r = state["ring"]
            state["ring"] = (r + 1) % 4
            size = at[1]
            lhs = augment(xb[slot, :, at[0]:at[0] + size], False).T
            rows = lax.broadcasted_iota(jnp.int32, (16, size), 0)
            vv = jnp.where(rows == team, jnp.broadcast_to(vb[slot, :, at[0]:at[0] + size].astype(jnp.float32), (16, size)), 0.0).astype(jnp.bfloat16)
            d = jnp.dot(lhs, wb[0:96, :], preferred_element_type=jnp.float32)
            kern = jnp.exp2(d * alpha).astype(jnp.bfloat16)
            fb[...] += jnp.dot(vv, kern, preferred_element_type=jnp.float32)

        def team_of(dx, dc):
            return 2 * (x + dx - 2 * x * dx) + c + dc - 2 * c * dc

        f1, f2, p1, p2 = 6 - c, 2 - c, 1 + c, 5 + c
        T = dict(own=team_of(0, 0), part=team_of(0, 1), f1=team_of(c, 1), p1=team_of(1 - c, 0), f2=team_of(c, 0), p2=team_of(1 - c, 1), d3=team_of(1, 0), d7=team_of(1, 1))
        whole = (0, N)

        tiles(0, T["own"], whole)
        flush()
        recv_v(4)
        sends.append(send_v(vb.at[4], 1 + c, 2, target))
        for k, at in enumerate(C1):
            recv_x(4, at, k)
            sends.append(send_x(xb.at[4], 1 + c, at, k, 2, target))
        tiles(4, T["part"], whole)
        flush()

        cond_sends = []
        nk = len(C1)
        later = []
        recv_v(f1)
        for k, at in enumerate(C1):
            recv_x(f1, at, k)
            if k == 0:
                sends.append(send_v(vb.at[f1], 7 - 4 * c, 3, third))
                sends.append(send_v(vb.at[f1], 2 - c, 4, partner))
            sends.append(send_x(xb.at[f1], 2 - c, at, k, 4, partner))
            for k3, at3 in enumerate(C3):
                if at[0] < at3[0] + at3[1] <= at[0] + at[1]:
                    sends.append(send_x(xb.at[f1], 7 - 4 * c, at3, k3, 3, third))
            tiles(f1, T["f1"], at)
            if k > 0:
                recv_x(p1, C1[k - 1], k - 1)
                if k == 1:
                    recv_v(p1)
                tiles(p1, T["p1"], C1[k - 1])
            flush()
        recv_v(f2)
        sends.append(send_v(vb.at[f2], 6 - c, 5, partner))
        for k, at in enumerate(C1):
            recv_x(f2, at, k)
            sends.append(send_x(xb.at[f2], 6 - c, at, k, 5, partner))
            tiles(f2, T["f2"], at)
            if k == 0:
                recv_x(p1, C1[-1], nk - 1)
                if nk == 1:
                    recv_v(p1)
                tiles(p1, T["p1"], C1[-1])
            else:
                recv_x(p2, C1[k - 1], k - 1)
                if k == 1:
                    recv_v(p2)
                tiles(p2, T["p2"], C1[k - 1])
            flush()
        recv_x(p2, C1[-1], nk - 1)
        if nk == 1:
            recv_v(p2)
        tiles(p2, T["p2"], C1[-1])
        flush()
        for k, at in enumerate(C3):
            recv_x(3, at, k)
            recv_x(7, at, k)
            if k == 0:
                recv_v(3)
                recv_v(7)

            @pl.when(c == 0)
            def _():
                if k == 0:
                    send_v(vb.at[3], 7, 6, partner)
                    send_v(vb.at[7], 3, 7, partner)
                send_x(xb.at[3], 7, at, k, 6, partner)
                send_x(xb.at[7], 3, at, k, 7, partner)

            tiles(3, T["d3"], at)
            tiles(7, T["d7"], at)
            flush()

        loads[2].wait()
        weight = jnp.sum(jnp.where(lax.broadcasted_iota(jnp.int32, (4, 4), 1) == t, mb[...].astype(jnp.float32), 0.0), axis=1, keepdims=True)
        o_ref[...] = jnp.sum(fb[0:4] * weight, axis=0, keepdims=True)

        for z in sends:
            z.wait_send()

        @pl.when(c == 0)
        def _():
            for k, at in enumerate(C3):
                cols = pl.ds(at[0], at[1])
                for s, lane in ((3, 6), (7, 7)):
                    remote(xb.at[s, :, cols], xb.at[10 - s, :, cols], send_sem.at[lane, k], recv_sem.at[10 - s, k], partner).wait_send()
            for s, lane in ((3, 6), (7, 7)):
                remote(vb.at[s], vb.at[10 - s], vsend_sem.at[lane], vrecv_sem.at[10 - s], partner).wait_send()

    compute(None)


def solution(mesh):
    spec = P(("dp", "team", "rep"), None)

    def per_device(points, values, pair_mask, bandwidth):
        hbm = [pltpu.with_memory_space_constraint(z, pltpu.HBM) for z in (points.T, values.T, pair_mask)]
        field = pl.pallas_call(
            kernel,
            out_shape=jax.ShapeDtypeStruct((1, N), jnp.float32),
            in_specs=[pl.BlockSpec(memory_space=pltpu.HBM)] * 3 + [pl.BlockSpec(memory_space=pltpu.SMEM)],
            out_specs=pl.BlockSpec(memory_space=pltpu.VMEM),
            scratch_shapes=[
                pltpu.VMEM((8, 90, N), jnp.bfloat16),
                pltpu.VMEM((8, 1, N), jnp.bfloat16),
                pltpu.VMEM((4, 4), jnp.int32),
                pltpu.VMEM((256, N), jnp.bfloat16),
                pltpu.VMEM((4, SUB, 256), jnp.bfloat16),
                pltpu.VMEM((16, N), jnp.float32),
                pltpu.SemaphoreType.DMA((3,)),
                pltpu.SemaphoreType.DMA((8, NK)),
                pltpu.SemaphoreType.DMA((8, NK)),
                pltpu.SemaphoreType.DMA((8,)),
                pltpu.SemaphoreType.DMA((8,)),
            ],
            compiler_params=pltpu.CompilerParams(collective_id=0, has_side_effects=True, vmem_limit_bytes=16 * 2**20),
        )(*hbm, bandwidth)
        return field.T

    return jax.shard_map(per_device, mesh=mesh, in_specs=(spec, spec, P("dp", None), P()), out_specs=spec, check_vma=False)
```

time: 71.6 us -> 16.1 us (0.22)
  the two profiles are of different devices: /device:TPU:0 before, /device:TPU:1 now
where the time goes in v1:
time: 16.1 us; the launch traced here: 16 us
  Pallas kernels  14.8 us (92%)
  between operations  0.66 us (4%)
  local copies, waits for them, and re-layouts  0.6 us (4%)
    pallas_call x1, Pallas kernels, per_device(): pl.pallas_call(kernel, out_shape=jax.ShapeDtypeStruct((1, N), jnp.float32...  14.8 us
    unnamed x1, local copies, waits for them, and re-layouts  0.6 us

profile of v1, /device:TPU:1, one launch (start us, length us, event | category | flops | bytes accessed | tf_op | source)
XLA Modules:
  0.0 16.0 jit_solution(12587028398768544932)
XLA Ops:
  0.7 14.8 %shard_map.46 = f32[1,1024]{1,0:T(1,128)S(1)} custom-call(bf16[90,1024]{1,0:T(8,128)(2,1)} %bitcast.4, bf16[1,1024]{1,0:T(2,128)(2,1)} %bitcast.5, s32[4,4]{1,0:T(4,128)} %m_hbm.1, f32[1]{0:T(128)S(6)} %copy.6.h_ref), custom_call_target="tpu_custom_call" | custom-call | tf_op jit(solution)/shard_map/pallas_call | solution.py:225
  15.4 0.6 %copy.7 = f32[1024,1]{0,1:T(1,128)} copy(f32[1024,1]{0,1:T(1,128)S(1)} %bitcast.3) | data formatting | bytes 8192

commit v2 on v0

v2 whole, which is shorter than its diff:
```python
import functools

import jax
import jax.numpy as jnp
from jax import lax
from jax.experimental import pallas as pl
from jax.experimental.pallas import tpu as pltpu
from jax.sharding import PartitionSpec as P

MESH = pl.DeviceIdType.MESH
N = 1024
SUB = 256
LOG2E = 1.4426950408889634


def chunks(sizes):
    out, at = [], 0
    for size in sizes:
        out.append((at, size))
        at += size
    return out


C1 = chunks((512, 512))
C3 = chunks((512, 512))
NK = 4
NOW = 0
TF = 0
NOV = 0
NOCOMP = 0
TJ = 256
TI = 512
LAG = 2
MERGE = 0


def split3(s):
    hi = s.astype(jnp.bfloat16).astype(jnp.float32)
    rest = s - hi
    mid = rest.astype(jnp.bfloat16).astype(jnp.float32)
    return hi, mid, rest - mid


def augment(xt, weights):
    n = xt.shape[1]
    x32 = xt.astype(jnp.float32)
    hi, mid, lo = split3(jnp.sum(x32 * x32, axis=0, keepdims=True))
    last = jnp.concatenate([x32[80:90], jnp.zeros((6, n), jnp.float32)], axis=0)
    row = lax.broadcasted_iota(jnp.int32, (16, n), 0)
    if weights:
        tail = jnp.where(row < 10, -2.0 * last, jnp.where(row < 13, 1.0, jnp.where(row == 13, hi, jnp.where(row == 14, mid, lo))))
        return jnp.concatenate([(-2.0 * x32[:80]).astype(jnp.bfloat16), tail.astype(jnp.bfloat16)], axis=0)
    tail = jnp.where(row < 10, last, jnp.where(row >= 13, 1.0, jnp.where(row == 10, hi, jnp.where(row == 11, mid, lo))))
    return jnp.concatenate([xt[:80], tail.astype(jnp.bfloat16)], axis=0)


def kernel(x_hbm, v_hbm, m_hbm, h_ref, o_ref, xb, vb, mb, wb, fb, load_sem, send_sem, recv_sem, vsend_sem, vrecv_sem, ready, peer, go):
    y, t, dp = lax.axis_index("rep"), lax.axis_index("team"), lax.axis_index("dp")
    x, c = t // 2, t % 2

    def dev(dx, dy, dc):
        return (dp, y + dy - 2 * y * dy, 2 * (x + dx - 2 * x * dx) + c + dc - 2 * c * dc)

    dx = c + y - 2 * c * y
    partner, target, source = dev(0, 0, 1), dev(dx, 1 - dx, dx), dev(1 - dx, dx, 1 - dx)

    last_chip = x * y
    bar = pltpu.get_barrier_semaphore()

    @pl.when(y * (1 - c * (1 - x)) == 0)
    def _():
        pl.semaphore_signal(bar, inc=1, device_id=source, device_id_type=MESH)

    @pl.when(c == 1)
    def _():
        pl.semaphore_signal(bar, inc=1, device_id=partner, device_id_type=MESH)

    loads = [pltpu.make_async_copy(src, dst, load_sem.at[i]) for i, (src, dst) in enumerate(((x_hbm, xb.at[0]), (v_hbm, vb.at[0]), (m_hbm, mb)))]
    for z in loads:
        z.start()

    sends = []

    def remote(src, dst, ssem, rsem, d):
        return pltpu.make_async_remote_copy(src_ref=src, dst_ref=dst, send_sem=ssem, recv_sem=rsem, device_id=d, device_id_type=MESH)

    def send_x(src, slot, at, k, lane, d, start=True):
        cols = pl.ds(at[0], at[1])
        z = remote(src.at[:, cols], xb.at[slot, :, cols], send_sem.at[lane, k], recv_sem.at[slot, k], d)
        if start:
            z.start()
        return z

    def send_v(src, slot, lane, d, start=True):
        z = remote(src, vb.at[slot], vsend_sem.at[lane], vrecv_sem.at[slot], d)
        if NOV:
            return None
        if start:
            z.start()
        return z

    def recv_x(slot, at, k):
        ref = xb.at[slot, :, pl.ds(at[0], at[1])]
        remote(ref, ref, send_sem.at[0, k], recv_sem.at[slot, k], partner).wait_recv()

    def recv_v(slot):
        if not NOV:
            remote(vb.at[slot], vb.at[slot], vsend_sem.at[0], vrecv_sem.at[slot], partner).wait_recv()

    def compute(accs):
        fb[...] = jnp.zeros_like(fb)
        def tiles(*parts):
            total, pend = {}, []
            ctx = jax.named_scope('tiles'); ctx.__enter__()
            if NOCOMP == 1 or (NOCOMP == 2 and parts[-1][0] != 7) or (NOCOMP==3 and parts[-1][0]==7):
                ctx.__exit__(None, None, None); return

            def drain():
                i, vv, d = pend.pop(0)
                kern = jnp.exp2(d * alpha).astype(jnp.bfloat16)
                r = jnp.dot(vv, kern, preferred_element_type=jnp.float32)
                total[i] = total[i] + r if i in total else r

            for slot, team, at in parts:
                lhs = augment(xb[slot, :, at[0]:at[0] + at[1]], False).T
                for j in range(0, at[1], TJ):
                    rows = lax.broadcasted_iota(jnp.int32, (16, TJ), 0)
                    v32 = vb[slot, :, at[0] + j:at[0] + j + TJ].astype(jnp.float32)
                    vv = jnp.where(rows == team, jnp.broadcast_to(v32, (16, TJ)), 0.0).astype(jnp.bfloat16)
                    for i in range(0, N, TI):
                        pend.append((i, vv, jnp.dot(lhs[j:j + TJ], wb[0:96, i:i + TI], preferred_element_type=jnp.float32)))
                        if len(pend) > LAG:
                            drain()
            while pend:
                drain()
            for i in total:
                fb[:, i:i + TI] += total[i]
            ctx.__exit__(None, None, None)

        def team_of(dx, dc):
            return 2 * (x + dx - 2 * x * dx) + c + dc - 2 * c * dc

        f1, f2, p1, p2 = 5 - 3 * dx, 1 + 5 * dx, 6 - 5 * dx, 2 + 3 * dx
        T = dict(own=team_of(0, 0), part=team_of(0, 1), f1=team_of(1 - dx, 1 - dx), f2=team_of(1 - dx, dx), p1=team_of(dx, 1 - dx), p2=team_of(dx, dx), d3=team_of(1, 0), d7=team_of(1, 1))

        def arrive(slot, k, ats, name='?'):
          with jax.named_scope(f'{name}{k}'):
            if k == 0:
                recv_v(slot)
            recv_x(slot, ats[k], k)

        def pass_on(slot, to, k, lane, d, ats):
            if k == 0:
                sends.append(send_v(vb.at[slot], to, lane, d))
            sends.append(send_x(xb.at[slot], to, ats[k], k, lane, d))

        n1, n3 = len(C1), len(C3)

        def got_first(k):
            arrive(f1, k, C1, 'f1_')
            end = C1[k][0] + C1[k][1]
            pass_on(f1, 1 + 5 * dx, k, 4, partner, C1)
            for k3, at3 in enumerate(C3):
                if C1[k][0] < at3[0] + at3[1] <= end:
                    pass_on(f1, 7, k3, 3, target, C3)
            return f1, T["f1"], C1[k]

        def got_second(k):
            arrive(f2, k, C1, 'f2_')
            pass_on(f2, 5 - 3 * dx, k, 5, partner, C1)
            return f2, T["f2"], C1[k]

        def got_p1(k):
            arrive(p1, k, C1, 'p1_')
            return p1, T["p1"], C1[k]

        def got_p2(k):
            arrive(p2, k, C1, 'p2_')
            return p2, T["p2"], C1[k]

        def got_third(k):
            arrive(7, k, C3, 'd7_')
            pass_on(7, 3, k, 6, partner, C3)
            return 7, T["d7"], C3[k]

        def got_last(k):
            arrive(3, k, C3, 'd3_')
            return 3, T["d3"], C3[k]

        alpha = -LOG2E / h_ref[0]

        def prepare():
            loads[0].wait()
            loads[1].wait()
            loads[2].wait()
            for i in range(0, N, SUB):
                wb[0:96, i:i + SUB] = augment(xb[0, :, i:i + SUB], True)

        first_chip = (1 - x) * (1 - y)

        @pl.when(first_chip == 1)
        def _():
            prepare()
            tiles((0, T["own"], (0, N)))

        with jax.named_scope('bar'):
            pl.semaphore_wait(bar, 1 + last_chip * (1 - c))

        def own_to_link(start):
            for k, at in enumerate(C1):
                z = send_x(x_hbm, 2 + 3 * dx, at, k, 0, target, start)
                zv = send_v(v_hbm, 2 + 3 * dx, 0, target, start) if k == 0 else None
                if not start:
                    z.wait_send()
                    if zv is not None:
                        zv.wait_send()

        direct = jnp.maximum(c, last_chip)

        @pl.when(direct == 1)
        def _():
            own_to_link(True)

        @pl.when(c == 0)
        def _():
            pl.semaphore_signal(ready, inc=1, device_id=partner, device_id_type=MESH)

        @pl.when(c == 1)
        def _():
            pl.semaphore_wait(ready, 1)

        @pl.when(y * (1 - (1 - x) * (1 - c)) == 1)
        def _():
            pl.semaphore_signal(peer, inc=1, device_id=target, device_id_type=MESH)

        for k, at in enumerate(C1):
            sends.append(send_x(x_hbm, 4, at, k, 1, partner))
        sends.append(send_v(v_hbm, 4, 1, partner))
        @pl.when(first_chip == 0)
        def _():
            prepare()

        @pl.when(c * (1 - last_chip) == 1)
        def _():
            with jax.named_scope('peer'):
                pl.semaphore_wait(peer, 1)
            pl.semaphore_signal(go, inc=1, device_id=partner, device_id_type=MESH)

        @pl.when(direct == 0)
        def _():
            with jax.named_scope('go'):
                pl.semaphore_wait(go, 1)
            own_to_link(True)

        for k in range(n1):
            arrive(4, k, C1, 'own4_')
            pass_on(4, 6 - 5 * dx, k, 2, target, C1)

        @pl.when(first_chip == 0)
        def _():
            tiles((0, T["own"], (0, N)))

        tiles((4, T["part"], (0, N)))
        weight = jnp.sum(jnp.where(lax.broadcasted_iota(jnp.int32, (4, 4), 1) == t, mb[...].astype(jnp.float32), 0.0), axis=1, keepdims=True)
        events = [[(got_first, 0)]]
        queue = [(got_first, k) for k in range(1, n1)] + [(got_second, k) for k in range(n1)]
        behind = [(got_p1, k) for k in range(n1)] + [(got_p2, k) for k in range(n1)]
        while queue:
            events.append([queue.pop(0), behind.pop(0)])
        events.append([behind.pop(0)])
        tail = ['70','71','30','31']
        for g in tail:
            events.append([((got_third if g[m] == '7' else got_last), int(g[m + 1])) for m in range(0, len(g), 2)])
        for group in events:
            parts = []
            for got, k in group:
                r = got(k)
                parts += r if isinstance(r[0], tuple) else [r]
            tiles(*parts)

        o_ref[...] = jnp.sum(fb[0:4] * weight, axis=0, keepdims=True)

        own_to_link(False)
        with jax.named_scope('sendw'):
          for z in sends:
            if z is not None:
                z.wait_send()

    compute(None)


def solution(mesh):
    spec = P(("dp", "team", "rep"), None)

    def per_device(points, values, pair_mask, bandwidth):
        hbm = [pltpu.with_memory_space_constraint(z, pltpu.HBM) for z in (points.T, values.T, pair_mask)]
        field = pl.pallas_call(
            kernel,
            out_shape=jax.ShapeDtypeStruct((1, N), jnp.float32),
            in_specs=[pl.BlockSpec(memory_space=pltpu.HBM)] * 3 + [pl.BlockSpec(memory_space=pltpu.SMEM)],
            out_specs=pl.BlockSpec(memory_space=pltpu.VMEM),
            scratch_shapes=[
                pltpu.VMEM((8, 90, N), jnp.bfloat16),
                pltpu.VMEM((8, 1, N), jnp.bfloat16),
                pltpu.VMEM((4, 4), jnp.int32),
                pltpu.VMEM((96, N), jnp.bfloat16),
                pltpu.VMEM((16, N), jnp.float32),
                pltpu.SemaphoreType.DMA((3,)),
                pltpu.SemaphoreType.DMA((8, NK)),
                pltpu.SemaphoreType.DMA((8, NK)),
                pltpu.SemaphoreType.DMA((8,)),
                pltpu.SemaphoreType.DMA((8,)),
                pltpu.SemaphoreType.REGULAR,
                pltpu.SemaphoreType.REGULAR,
                pltpu.SemaphoreType.REGULAR,
            ],
            compiler_params=pltpu.CompilerParams(collective_id=0, has_side_effects=True, vmem_limit_bytes=16 * 2**20),
        )(*hbm, bandwidth)
        return field.T

    return jax.shard_map(per_device, mesh=mesh, in_specs=(spec, spec, P("dp", None), P()), out_specs=spec, check_vma=False)
```

time: 71.6 us -> 14.6 us (0.20)
  the two profiles are of different devices: /device:TPU:0 before, /device:TPU:5 now
where the time goes in v2:
time: 14.6 us; the launch traced here: 14.5 us
  Pallas kernels  13.3 us (91%)
  between operations  0.66 us (5%)
  local copies, waits for them, and re-layouts  0.6 us (4%)
    pallas_call x1, Pallas kernels, per_device(): pl.pallas_call(kernel, out_shape=jax.ShapeDtypeStruct((1, N), jnp.float32...  13.3 us
    unnamed x1, local copies, waits for them, and re-layouts  0.6 us

profile of v2, /device:TPU:5, one launch (start us, length us, event | category | flops | bytes accessed | tf_op | source)
XLA Modules:
  0.0 14.5 jit_solution(8248964048515071982)
XLA Ops:
  0.7 13.3 %shard_map.46 = f32[1,1024]{1,0:T(1,128)S(1)} custom-call(bf16[90,1024]{1,0:T(8,128)(2,1)} %bitcast.4, bf16[1,1024]{1,0:T(2,128)(2,1)} %bitcast.5, s32[4,4]{1,0:T(4,128)} %m_hbm.1, f32[1]{0:T(128)S(6)} %copy.6.h_ref), custom_call_target="tpu_custom_call" | custom-call | tf_op jit(solution)/shard_map/pallas_call | solution.py:297
  13.9 0.6 %copy.7 = f32[1024,1]{0,1:T(1,128)} copy(f32[1024,1]{0,1:T(1,128)S(1)} %bitcast.3) | data formatting | bytes 8192

commit v3 on v0

v3 whole, which is shorter than its diff:
```python
import functools

import jax
import jax.numpy as jnp
from jax import lax
from jax.experimental import pallas as pl
from jax.experimental.pallas import tpu as pltpu
from jax.sharding import PartitionSpec as P

MESH = pl.DeviceIdType.MESH
N = 1024
LOG2E = 1.4426950408889634
TJ = 256
TI = 512
LAG = 3
SCOPED = 1
NOCOMP = 0
HALVES = ((0, 512), (512, 512))


def split3(s):
    hi = s.astype(jnp.bfloat16).astype(jnp.float32)
    rest = s - hi
    mid = rest.astype(jnp.bfloat16).astype(jnp.float32)
    return hi, mid, rest - mid


def augment(xt, weights):
    n = xt.shape[1]
    x32 = xt.astype(jnp.float32)
    hi, mid, lo = split3(jnp.sum(x32 * x32, axis=0, keepdims=True))
    last = jnp.concatenate([x32[80:90], jnp.zeros((6, n), jnp.float32)], axis=0)
    row = lax.broadcasted_iota(jnp.int32, (16, n), 0)
    if weights:
        tail = jnp.where(row < 10, -2.0 * last, jnp.where(row < 13, 1.0, jnp.where(row == 13, hi, jnp.where(row == 14, mid, lo))))
        return jnp.concatenate([(-2.0 * x32[:80]).astype(jnp.bfloat16), tail.astype(jnp.bfloat16)], axis=0)
    tail = jnp.where(row < 10, last, jnp.where(row >= 13, 1.0, jnp.where(row == 10, hi, jnp.where(row == 11, mid, lo))))
    return jnp.concatenate([xt[:80], tail.astype(jnp.bfloat16)], axis=0)


def body(x_hbm, v_hbm, m_hbm, h_ref, o_ref, xb, vb, mb, wb, fb, load_sem, sent_x, sent_v, got_x, got_v, note, peer):
    y, t, dp = lax.axis_index("rep"), lax.axis_index("team"), lax.axis_index("dp")
    x, c = t // 2, t % 2
    dx = c + y - 2 * c * y
    odd = x + y - 2 * x * y
    first_chip, last_chip = (1 - x) * (1 - y), x * y

    def dev(fx, fy, fc):
        return (dp, y + fy - 2 * y * fy, 2 * (x + fx - 2 * x * fx) + c + fc - 2 * c * fc)

    def team_of(fx, fc):
        return 2 * (x + fx - 2 * x * fx) + c + fc - 2 * c * fc

    partner, target, source = dev(0, 0, 1), dev(dx, 1 - dx, dx), dev(1 - dx, dx, 1 - dx)

    def signal(sem, d):
        pl.semaphore_signal(sem, inc=1, device_id=d, device_id_type=MESH)

    bar = pltpu.get_barrier_semaphore()
    pl.when(last_chip == 0)(lambda: signal(bar, source))
    pl.when(jnp.maximum(c, 1 - odd) == 1)(lambda: signal(bar, partner))
    loads = [pltpu.make_async_copy(src, dst, load_sem.at[i]) for i, (src, dst) in enumerate(((x_hbm, xb.at[0]), (v_hbm, vb.at[0]), (m_hbm, mb)))]
    for z in loads:
        z.start()
    fb[...] = jnp.zeros_like(fb)

    def copy_x(src, dst, slot, k, d):
        return pltpu.make_async_remote_copy(src_ref=src, dst_ref=dst, send_sem=sent_x, recv_sem=got_x.at[slot - 1, k], device_id=d, device_id_type=MESH)

    def copy_v(src, slot, d):
        return pltpu.make_async_remote_copy(src_ref=src, dst_ref=vb.at[slot], send_sem=sent_v, recv_sem=got_v.at[slot - 1], device_id=d, device_id_type=MESH)

    def send(x_src, v_src, slot, k, d):
        cols = pl.ds(*HALVES[k])
        copy_x(x_src.at[:, cols], xb.at[slot, :, cols], slot, k, d).start()
        if k == 0:
            copy_v(v_src, slot, d).start()

    def pass_on(slot, to, k, d):
        send(xb.at[slot], vb.at[slot], to, k, d)

    def arrive(slot, k, name):
        with jax.named_scope(f"{name}{k}"):
            if k == 0:
                copy_v(vb.at[slot], slot, partner).wait_recv()
            ref = xb.at[slot, :, pl.ds(*HALVES[k])]
            copy_x(ref, ref, slot, k, partner).wait_recv()

    alpha = -LOG2E / h_ref[0]

    def tiles(*parts):
        if NOCOMP:
            return
        total, pend = {}, []

        def drain():
            i, vv, d = pend.pop(0)
            kern = jnp.exp2(d * alpha).astype(jnp.bfloat16)
            r = jnp.dot(vv, kern, preferred_element_type=jnp.float32)
            total[i] = total[i] + r if i in total else r

        with jax.named_scope("tiles"):
            for slot, team, at in parts:
                lhs = augment(xb[slot, :, at[0]:at[0] + at[1]], False).T
                for j in range(0, at[1], TJ):
                    rows = lax.broadcasted_iota(jnp.int32, (16, TJ), 0)
                    v32 = vb[slot, :, at[0] + j:at[0] + j + TJ].astype(jnp.float32)
                    vv = jnp.where(rows == team, jnp.broadcast_to(v32, (16, TJ)), 0.0).astype(jnp.bfloat16)
                    for i in range(0, N, TI):
                        pend.append((i, vv, jnp.dot(lhs[j:j + TJ], wb[:, i:i + TI], preferred_element_type=jnp.float32)))
                        if len(pend) > LAG:
                            drain()
            while pend:
                drain()
            for i in total:
                fb[:, i:i + TI] += total[i]

    def prepare():
        for z in loads:
            z.wait()
        for i in range(0, N, 256):
            wb[:, i:i + 256] = augment(xb[0, :, i:i + 256], True)

    def own_sum():
        tiles((0, team_of(0, 0), (0, N)))

    def own_to(slot, d):
        for k in range(2):
            send(x_hbm, v_hbm, slot, k, d)

    @pl.when(first_chip == 1)
    def _():
        prepare()
        own_sum()

    with jax.named_scope("bar"):
        pl.semaphore_wait(bar, 2 - odd)
    pl.when(odd * (1 - c) == 1)(lambda: signal(note, partner))
    pl.when(last_chip == 1)(lambda: signal(peer, target))

    @pl.when(jnp.maximum(c, 1 - odd) == 1)
    def _():
        own_to(2 + 3 * dx, target)

    @pl.when(odd * c == 1)
    def _():
        pl.semaphore_wait(note, 1)

    own_to(4, partner)

    @pl.when(first_chip == 0)
    def _():
        prepare()

    @pl.when(odd * c == 1)
    def _():
        with jax.named_scope("peer"):
            pl.semaphore_wait(peer, 1)
        signal(note, partner)

    @pl.when(odd * (1 - c) == 1)
    def _():
        with jax.named_scope("go"):
            pl.semaphore_wait(note, 1)
        own_to(2 + 3 * dx, target)

    for k in range(2):
        arrive(4, k, "own4_")
        pass_on(4, 6 - 5 * dx, k, target)

    pl.when(first_chip == 0)(own_sum)
    tiles((4, team_of(0, 1), (0, N)))
    weight = jnp.sum(jnp.where(lax.broadcasted_iota(jnp.int32, (4, 4), 1) == t, mb[...].astype(jnp.float32), 0.0), axis=1, keepdims=True)

    f1, f2, p1, p2 = 5 - 3 * dx, 1 + 5 * dx, 6 - 5 * dx, 2 + 3 * dx

    def first(k):
        arrive(f1, k, "f1_")
        pass_on(f1, 1 + 5 * dx, k, partner)
        pass_on(f1, 7, k, target)
        return f1, team_of(1 - dx, 1 - dx), HALVES[k]

    def second(k):
        arrive(f2, k, "f2_")
        pass_on(f2, 5 - 3 * dx, k, partner)
        return f2, team_of(1 - dx, dx), HALVES[k]

    def third(k):
        arrive(7, k, "d7_")
        pass_on(7, 3, k, partner)
        return 7, team_of(1, 1), HALVES[k]

    def first_behind(k):
        arrive(p1, k, "p1_")
        return p1, team_of(dx, 1 - dx), HALVES[k]

    def second_behind(k):
        arrive(p2, k, "p2_")
        return p2, team_of(dx, dx), HALVES[k]

    def third_behind(k):
        arrive(3, k, "d3_")
        return 3, team_of(1, 0), HALVES[k]

    ahead = [(got, k) for got in (first, second, third) for k in range(2)]
    behind = [(got, k) for got in (first_behind, second_behind, third_behind) for k in range(2)]
    for g in range(7):
        group = ahead[g:g + 1] + (behind[g - 1:g] if g else [])
        tiles(*[got(k) for got, k in group])

    o_ref[...] = jnp.sum(fb[0:4] * weight, axis=0, keepdims=True)
    with jax.named_scope("sendw"):
        copy_x(xb.at[0:7], xb.at[1:8], 1, 0, partner).wait_send()
        copy = pltpu.make_async_remote_copy(src_ref=vb.at[0:7], dst_ref=vb.at[1:8], send_sem=sent_v, recv_sem=got_v.at[0], device_id=partner, device_id_type=MESH)
        copy.wait_send()


SEMS = [
    pltpu.SemaphoreType.DMA((3,)),
    pltpu.SemaphoreType.DMA,
    pltpu.SemaphoreType.DMA,
    pltpu.SemaphoreType.DMA((7, 2)),
    pltpu.SemaphoreType.DMA((7,)),
    pltpu.SemaphoreType.REGULAR,
    pltpu.SemaphoreType.REGULAR,
]


def kernel(*refs):
    if SCOPED:
        pl.run_scoped(functools.partial(body, *refs), *SEMS)
    else:
        body(*refs)


def solution(mesh):
    spec = P(("dp", "team", "rep"), None)

    def per_device(points, values, pair_mask, bandwidth):
        hbm = [pltpu.with_memory_space_constraint(z, pltpu.HBM) for z in (points.T, values.T, pair_mask)]
        field = pl.pallas_call(
            kernel,
            out_shape=jax.ShapeDtypeStruct((1, N), jnp.float32),
            in_specs=[pl.BlockSpec(memory_space=pltpu.HBM)] * 3 + [pl.BlockSpec(memory_space=pltpu.SMEM)],
            out_specs=pl.BlockSpec(memory_space=pltpu.VMEM),
            scratch_shapes=[
                pltpu.VMEM((8, 90, N), jnp.bfloat16),
                pltpu.VMEM((8, 1, N), jnp.bfloat16),
                pltpu.VMEM((4, 4), jnp.int32),
                pltpu.VMEM((96, N), jnp.bfloat16),
                pltpu.VMEM((16, N), jnp.float32),
                *(() if SCOPED else SEMS),
            ],
            compiler_params=pltpu.CompilerParams(collective_id=0, has_side_effects=True, vmem_limit_bytes=16 * 2**20),
        )(*hbm, bandwidth)
        return field.T

    return jax.shard_map(per_device, mesh=mesh, in_specs=(spec, spec, P("dp", None), P()), out_specs=spec, check_vma=False)
```

time: 71.6 us -> 13.8 us (0.19)
  the two profiles are of different devices: /device:TPU:0 before, /device:TPU:7 now
where the time goes in v3:
time: 13.8 us; the launch traced here: 13.7 us
  Pallas kernels  12.4 us (90%)
  between operations  0.66 us (5%)
  local copies, waits for them, and re-layouts  0.6 us (4%)
    pallas_call x1, Pallas kernels, per_device(): pl.pallas_call(kernel, out_shape=jax.ShapeDtypeStruct((1, N), jnp.float32...  12.4 us
    unnamed x1, local copies, waits for them, and re-layouts  0.6 us

profile of v3, /device:TPU:7, one launch (start us, length us, event | category | flops | bytes accessed | tf_op | source)
XLA Modules:
  0.0 13.7 jit_solution(3297898995344966349)
XLA Ops:
  0.7 12.4 %shard_map.46 = f32[1,1024]{1,0:T(1,128)S(1)} custom-call(bf16[90,1024]{1,0:T(8,128)(2,1)} %bitcast.4, bf16[1,1024]{1,0:T(2,128)(2,1)} %bitcast.5, s32[4,4]{1,0:T(4,128)} %refs_2_.1, f32[1]{0:T(128)S(6)} %copy.6.refs_3_), custom_call_target="tpu_custom_call" | custom-call | tf_op jit(solution)/shard_map/pallas_call | solution.py:241
  13.1 0.6 %copy.7 = f32[1024,1]{0,1:T(1,128)} copy(f32[1024,1]{0,1:T(1,128)S(1)} %bitcast.3) | data formatting | bytes 8192

commit v4 on v3

--- a/solution.py
+++ b/solution.py
@@ -14,6 +14,9 @@
 TI = 512
 LAG = 3
 SCOPED = 1
+LTJ = 512
+LTI = 512
+LLAG = 1
 NOCOMP = 0
 HALVES = ((0, 512), (512, 512))
 
@@ -25,11 +28,12 @@
     return hi, mid, rest - mid
 
 
-def augment(xt, weights):
+def augment(xt, rest, weights):
     n = xt.shape[1]
     x32 = xt.astype(jnp.float32)
-    hi, mid, lo = split3(jnp.sum(x32 * x32, axis=0, keepdims=True))
-    last = jnp.concatenate([x32[80:90], jnp.zeros((6, n), jnp.float32)], axis=0)
+    r32 = rest.astype(jnp.float32)
+    hi, mid, lo = split3(jnp.sum(x32 * x32, axis=0, keepdims=True) + jnp.sum(r32 * r32, axis=0, keepdims=True))
+    last = jnp.concatenate([x32[80:88], r32, jnp.zeros((6, n), jnp.float32)], axis=0)
     row = lax.broadcasted_iota(jnp.int32, (16, n), 0)
     if weights:
         tail = jnp.where(row < 10, -2.0 * last, jnp.where(row < 13, 1.0, jnp.where(row == 13, hi, jnp.where(row == 14, mid, lo))))
@@ -38,7 +42,7 @@
     return jnp.concatenate([xt[:80], tail.astype(jnp.bfloat16)], axis=0)
 
 
-def body(x_hbm, v_hbm, m_hbm, h_ref, o_ref, xb, vb, mb, wb, fb, load_sem, sent_x, sent_v, got_x, got_v, note, peer):
+def body(x_hbm, v_hbm, m_hbm, h_ref, o_ref, xb, rb, vb, mb, wb, fb, load_sem, sent_x, sent_r, sent_v, got_x, got_r, got_v, note, peer):
     y, t, dp = lax.axis_index("rep"), lax.axis_index("team"), lax.axis_index("dp")
     x, c = t // 2, t % 2
     dx = c + y - 2 * c * y
@@ -59,36 +63,40 @@
     bar = pltpu.get_barrier_semaphore()
     pl.when(last_chip == 0)(lambda: signal(bar, source))
     pl.when(jnp.maximum(c, 1 - odd) == 1)(lambda: signal(bar, partner))
-    loads = [pltpu.make_async_copy(src, dst, load_sem.at[i]) for i, (src, dst) in enumerate(((x_hbm, xb.at[0]), (v_hbm, vb.at[0]), (m_hbm, mb)))]
+    loads = [pltpu.make_async_copy(src, dst, load_sem.at[i]) for i, (src, dst) in enumerate(((x_hbm.at[0:88], xb.at[0]), (x_hbm.at[88:90], rb.at[0]), (v_hbm, vb.at[0]), (m_hbm, mb)))]
     for z in loads:
         z.start()
-    fb[...] = jnp.zeros_like(fb)
-
     def copy_x(src, dst, slot, k, d):
         return pltpu.make_async_remote_copy(src_ref=src, dst_ref=dst, send_sem=sent_x, recv_sem=got_x.at[slot - 1, k], device_id=d, device_id_type=MESH)
 
     def copy_v(src, slot, d):
         return pltpu.make_async_remote_copy(src_ref=src, dst_ref=vb.at[slot], send_sem=sent_v, recv_sem=got_v.at[slot - 1], device_id=d, device_id_type=MESH)
 
-    def send(x_src, v_src, slot, k, d):
+    def copy_r(src, slot, d):
+        return pltpu.make_async_remote_copy(src_ref=src, dst_ref=rb.at[slot], send_sem=sent_r, recv_sem=got_r.at[slot - 1], device_id=d, device_id_type=MESH)
+
+    def send(x_src, r_src, v_src, slot, k, d):
         cols = pl.ds(*HALVES[k])
+        if k == 0:
+            copy_r(r_src, slot, d).start()
         copy_x(x_src.at[:, cols], xb.at[slot, :, cols], slot, k, d).start()
         if k == 0:
             copy_v(v_src, slot, d).start()
 
     def pass_on(slot, to, k, d):
-        send(xb.at[slot], vb.at[slot], to, k, d)
+        send(xb.at[slot], rb.at[slot], vb.at[slot], to, k, d)
 
     def arrive(slot, k, name):
         with jax.named_scope(f"{name}{k}"):
             if k == 0:
                 copy_v(vb.at[slot], slot, partner).wait_recv()
+                copy_r(rb.at[slot], slot, partner).wait_recv()
             ref = xb.at[slot, :, pl.ds(*HALVES[k])]
             copy_x(ref, ref, slot, k, partner).wait_recv()
 
     alpha = -LOG2E / h_ref[0]
 
-    def tiles(*parts):
+    def tiles(*parts, tj=TJ, ti=TI, lag=LAG):
         if NOCOMP:
             return
         total, pend = {}, []
@@ -101,32 +109,33 @@
 
         with jax.named_scope("tiles"):
             for slot, team, at in parts:
-                lhs = augment(xb[slot, :, at[0]:at[0] + at[1]], False).T
-                for j in range(0, at[1], TJ):
-                    rows = lax.broadcasted_iota(jnp.int32, (16, TJ), 0)
-                    v32 = vb[slot, :, at[0] + j:at[0] + j + TJ].astype(jnp.float32)
-                    vv = jnp.where(rows == team, jnp.broadcast_to(v32, (16, TJ)), 0.0).astype(jnp.bfloat16)
-                    for i in range(0, N, TI):
-                        pend.append((i, vv, jnp.dot(lhs[j:j + TJ], wb[:, i:i + TI], preferred_element_type=jnp.float32)))
-                        if len(pend) > LAG:
+                lhs = augment(xb[slot, :, at[0]:at[0] + at[1]], rb[slot, :, at[0]:at[0] + at[1]], False).T
+                for j in range(0, at[1], tj):
+                    rows = lax.broadcasted_iota(jnp.int32, (16, tj), 0)
+                    v32 = vb[slot, :, at[0] + j:at[0] + j + tj].astype(jnp.float32)
+                    vv = jnp.where(rows == team, jnp.broadcast_to(v32, (16, tj)), 0.0).astype(jnp.bfloat16)
+                    for i in range(0, N, ti):
+                        pend.append((i, vv, jnp.dot(lhs[j:j + tj], wb[:, i:i + ti], preferred_element_type=jnp.float32)))
+                        if len(pend) > lag:
                             drain()
             while pend:
                 drain()
             for i in total:
-                fb[:, i:i + TI] += total[i]
+                fb[:, i:i + ti] += total[i]
 
     def prepare():
+        fb[...] = jnp.zeros_like(fb)
         for z in loads:
             z.wait()
         for i in range(0, N, 256):
-            wb[:, i:i + 256] = augment(xb[0, :, i:i + 256], True)
+            wb[:, i:i + 256] = augment(xb[0, :, i:i + 256], rb[0, :, i:i + 256], True)
 
     def own_sum():
         tiles((0, team_of(0, 0), (0, N)))
 
     def own_to(slot, d):
         for k in range(2):
-            send(x_hbm, v_hbm, slot, k, d)
+            send(x_hbm.at[0:88], x_hbm.at[88:90], v_hbm, slot, k, d)
 
     @pl.when(first_chip == 1)
     def _():
@@ -206,20 +215,27 @@
     behind = [(got, k) for got in (first_behind, second_behind, third_behind) for k in range(2)]
     for g in range(7):
         group = ahead[g:g + 1] + (behind[g - 1:g] if g else [])
-        tiles(*[got(k) for got, k in group])
+        parts = [got(k) for got, k in group]
+        if g < 6:
+            tiles(*parts)
+        else:
+            tiles(*parts, tj=LTJ, ti=LTI, lag=LLAG)
 
     o_ref[...] = jnp.sum(fb[0:4] * weight, axis=0, keepdims=True)
     with jax.named_scope("sendw"):
         copy_x(xb.at[0:7], xb.at[1:8], 1, 0, partner).wait_send()
+        pltpu.make_async_remote_copy(src_ref=rb.at[0:7], dst_ref=rb.at[1:8], send_sem=sent_r, recv_sem=got_r.at[0], device_id=partner, device_id_type=MESH).wait_send()
         copy = pltpu.make_async_remote_copy(src_ref=vb.at[0:7], dst_ref=vb.at[1:8], send_sem=sent_v, recv_sem=got_v.at[0], device_id=partner, device_id_type=MESH)
         copy.wait_send()
 
 
 SEMS = [
-    pltpu.SemaphoreType.DMA((3,)),
+    pltpu.SemaphoreType.DMA((4,)),
+    pltpu.SemaphoreType.DMA,
     pltpu.SemaphoreType.DMA,
     pltpu.SemaphoreType.DMA,
     pltpu.SemaphoreType.DMA((7, 2)),
+    pltpu.SemaphoreType.DMA((7,)),
     pltpu.SemaphoreType.DMA((7,)),
     pltpu.SemaphoreType.REGULAR,
     pltpu.SemaphoreType.REGULAR,
@@ -244,7 +260,8 @@
             in_specs=[pl.BlockSpec(memory_space=pltpu.HBM)] * 3 + [pl.BlockSpec(memory_space=pltpu.SMEM)],
             out_specs=pl.BlockSpec(memory_space=pltpu.VMEM),
             scratch_shapes=[
-                pltpu.VMEM((8, 90, N), jnp.bfloat16),
+                pltpu.VMEM((8, 88, N), jnp.bfloat16),
+                pltpu.VMEM((8, 2, N), jnp.bfloat16),
                 pltpu.VMEM((8, 1, N), jnp.bfloat16),
                 pltpu.VMEM((4, 4), jnp.int32),
                 pltpu.VMEM((96, N), jnp.bfloat16),

time: 13.8 us -> 13.4 us (0.971)
  the two profiles are of different devices: /device:TPU:7 before, /device:TPU:0 now
where the time goes in v4:
time: 13.4 us; the launch traced here: 13.2 us
  Pallas kernels  12 us (90%)
  between operations  0.66 us (5%)
  local copies, waits for them, and re-layouts  0.6 us (4%)
    pallas_call x1, Pallas kernels, per_device(): pl.pallas_call(kernel, out_shape=jax.ShapeDtypeStruct((1, N), jnp.float32...  12 us
    unnamed x1, local copies, waits for them, and re-layouts  0.6 us

profile of v4, /device:TPU:0, one launch (start us, length us, event | category | flops | bytes accessed | tf_op | source)
XLA Modules:
  0.0 13.2 jit_solution(17047524332039892257)
XLA Ops:
  0.7 12.0 %shard_map.46 = f32[1,1024]{1,0:T(1,128)S(1)} custom-call(bf16[90,1024]{1,0:T(8,128)(2,1)} %bitcast.4, bf16[1,1024]{1,0:T(2,128)(2,1)} %bitcast.5, s32[4,4]{1,0:T(4,128)} %refs_2_.1, f32[1]{0:T(128)S(6)} %copy.6.refs_3_), custom_call_target="tpu_custom_call" | custom-call | tf_op jit(solution)/shard_map/pallas_call | solution.py:257
  12.6 0.6 %copy.7 = f32[1024,1]{0,1:T(1,128)} copy(f32[1024,1]{0,1:T(1,128)S(1)} %bitcast.3) | data formatting | bytes 8192

commit v5 on v4

--- a/solution.py
+++ b/solution.py
@@ -10,14 +10,8 @@
 MESH = pl.DeviceIdType.MESH
 N = 1024
 LOG2E = 1.4426950408889634
-TJ = 256
-TI = 512
-LAG = 3
-SCOPED = 1
-LTJ = 512
-LTI = 512
-LLAG = 1
-NOCOMP = 0
+WIDE = 2.0**64
+TJ, TI, LAG = 512, 512, 1
 HALVES = ((0, 512), (512, 512))
 
 
@@ -28,16 +22,16 @@
     return hi, mid, rest - mid
 
 
-def augment(xt, rest, weights):
+def augment(xt, rest, scale=None):
     n = xt.shape[1]
     x32 = xt.astype(jnp.float32)
     r32 = rest.astype(jnp.float32)
     hi, mid, lo = split3(jnp.sum(x32 * x32, axis=0, keepdims=True) + jnp.sum(r32 * r32, axis=0, keepdims=True))
     last = jnp.concatenate([x32[80:88], r32, jnp.zeros((6, n), jnp.float32)], axis=0)
     row = lax.broadcasted_iota(jnp.int32, (16, n), 0)
-    if weights:
+    if scale is not None:
         tail = jnp.where(row < 10, -2.0 * last, jnp.where(row < 13, 1.0, jnp.where(row == 13, hi, jnp.where(row == 14, mid, lo))))
-        return jnp.concatenate([(-2.0 * x32[:80]).astype(jnp.bfloat16), tail.astype(jnp.bfloat16)], axis=0)
+        return jnp.concatenate([(-2.0 * scale * x32[:80]).astype(jnp.bfloat16), (scale * tail).astype(jnp.bfloat16)], axis=0)
     tail = jnp.where(row < 10, last, jnp.where(row >= 13, 1.0, jnp.where(row == 10, hi, jnp.where(row == 11, mid, lo))))
     return jnp.concatenate([xt[:80], tail.astype(jnp.bfloat16)], axis=0)
 
@@ -64,8 +58,13 @@
     pl.when(last_chip == 0)(lambda: signal(bar, source))
     pl.when(jnp.maximum(c, 1 - odd) == 1)(lambda: signal(bar, partner))
     loads = [pltpu.make_async_copy(src, dst, load_sem.at[i]) for i, (src, dst) in enumerate(((x_hbm.at[0:88], xb.at[0]), (x_hbm.at[88:90], rb.at[0]), (v_hbm, vb.at[0]), (m_hbm, mb)))]
-    for z in loads:
-        z.start()
+
+    def load():
+        for z in loads:
+            z.start()
+
+    pl.when(first_chip == 1)(load)
+
     def copy_x(src, dst, slot, k, d):
         return pltpu.make_async_remote_copy(src_ref=src, dst_ref=dst, send_sem=sent_x, recv_sem=got_x.at[slot - 1, k], device_id=d, device_id_type=MESH)
 
@@ -94,11 +93,10 @@
             ref = xb.at[slot, :, pl.ds(*HALVES[k])]
             copy_x(ref, ref, slot, k, partner).wait_recv()
 
-    alpha = -LOG2E / h_ref[0]
-
-    def tiles(*parts, tj=TJ, ti=TI, lag=LAG):
-        if NOCOMP:
-            return
+    scale = jnp.where(h_ref[0] > WIDE, 1.0 / WIDE, 1.0)
+    alpha = -LOG2E / (h_ref[0] * scale)
+
+    def tiles(*parts):
         total, pend = {}, []
 
         def drain():
@@ -109,26 +107,26 @@
 
         with jax.named_scope("tiles"):
             for slot, team, at in parts:
-                lhs = augment(xb[slot, :, at[0]:at[0] + at[1]], rb[slot, :, at[0]:at[0] + at[1]], False).T
-                for j in range(0, at[1], tj):
-                    rows = lax.broadcasted_iota(jnp.int32, (16, tj), 0)
-                    v32 = vb[slot, :, at[0] + j:at[0] + j + tj].astype(jnp.float32)
-                    vv = jnp.where(rows == team, jnp.broadcast_to(v32, (16, tj)), 0.0).astype(jnp.bfloat16)
-                    for i in range(0, N, ti):
-                        pend.append((i, vv, jnp.dot(lhs[j:j + tj], wb[:, i:i + ti], preferred_element_type=jnp.float32)))
-                        if len(pend) > lag:
+                lhs = augment(xb[slot, :, at[0]:at[0] + at[1]], rb[slot, :, at[0]:at[0] + at[1]]).T
+                for j in range(0, at[1], TJ):
+                    rows = lax.broadcasted_iota(jnp.int32, (16, TJ), 0)
+                    v32 = vb[slot, :, at[0] + j:at[0] + j + TJ].astype(jnp.float32)
+                    vv = jnp.where(rows == team, jnp.broadcast_to(v32, (16, TJ)), 0.0).astype(jnp.bfloat16)
+                    for i in range(0, N, TI):
+                        pend.append((i, vv, jnp.dot(lhs[j:j + TJ], wb[:, i:i + TI], preferred_element_type=jnp.float32)))
+                        if len(pend) > LAG:
                             drain()
             while pend:
                 drain()
             for i in total:
-                fb[:, i:i + ti] += total[i]
+                fb[:, i:i + TI] += total[i]
 
     def prepare():
         fb[...] = jnp.zeros_like(fb)
         for z in loads:
             z.wait()
         for i in range(0, N, 256):
-            wb[:, i:i + 256] = augment(xb[0, :, i:i + 256], rb[0, :, i:i + 256], True)
+            wb[:, i:i + 256] = augment(xb[0, :, i:i + 256], rb[0, :, i:i + 256], scale)
 
     def own_sum():
         tiles((0, team_of(0, 0), (0, N)))
@@ -144,12 +142,13 @@
 
     with jax.named_scope("bar"):
         pl.semaphore_wait(bar, 2 - odd)
+    @pl.when(jnp.maximum(c, 1 - odd) == 1)
+    def _():
+        own_to(2 + 3 * dx, target)
+
+    pl.when(last_chip == 1)(lambda: signal(peer, target))
     pl.when(odd * (1 - c) == 1)(lambda: signal(note, partner))
-    pl.when(last_chip == 1)(lambda: signal(peer, target))
-
-    @pl.when(jnp.maximum(c, 1 - odd) == 1)
-    def _():
-        own_to(2 + 3 * dx, target)
+    pl.when(first_chip == 0)(load)
 
     @pl.when(odd * c == 1)
     def _():
@@ -215,11 +214,7 @@
     behind = [(got, k) for got in (first_behind, second_behind, third_behind) for k in range(2)]
     for g in range(7):
         group = ahead[g:g + 1] + (behind[g - 1:g] if g else [])
-        parts = [got(k) for got, k in group]
-        if g < 6:
-            tiles(*parts)
-        else:
-            tiles(*parts, tj=LTJ, ti=LTI, lag=LLAG)
+        tiles(*[got(k) for got, k in group])
 
     o_ref[...] = jnp.sum(fb[0:4] * weight, axis=0, keepdims=True)
     with jax.named_scope("sendw"):
@@ -243,10 +238,7 @@
 
 
 def kernel(*refs):
-    if SCOPED:
-        pl.run_scoped(functools.partial(body, *refs), *SEMS)
-    else:
-        body(*refs)
+    pl.run_scoped(functools.partial(body, *refs), *SEMS)
 
 
 def solution(mesh):
@@ -266,7 +258,6 @@
                 pltpu.VMEM((4, 4), jnp.int32),
                 pltpu.VMEM((96, N), jnp.bfloat16),
                 pltpu.VMEM((16, N), jnp.float32),
-                *(() if SCOPED else SEMS),
             ],
             compiler_params=pltpu.CompilerParams(collective_id=0, has_side_effects=True, vmem_limit_bytes=16 * 2**20),
         )(*hbm, bandwidth)

time: 13.4 us -> 13.3 us (level)
  no operation moved by 1% of the time
where the time goes in v5:
time: 13.3 us; the launch traced here: 13.2 us
  Pallas kernels  12 us (90%)
  between operations  0.66 us (5%)
  local copies, waits for them, and re-layouts  0.6 us (5%)
    pallas_call x1, Pallas kernels, per_device(): pl.pallas_call(kernel, out_shape=jax.ShapeDtypeStruct((1, N), jnp.float32...  12 us
    unnamed x1, local copies, waits for them, and re-layouts  0.6 us

profile of v5, /device:TPU:0, one launch (start us, length us, event | category | flops | bytes accessed | tf_op | source)
XLA Modules:
  0.0 13.2 jit_solution(10305188954909751129)
XLA Ops:
  0.7 12.0 %shard_map.46 = f32[1,1024]{1,0:T(1,128)S(1)} custom-call(bf16[90,1024]{1,0:T(8,128)(2,1)} %bitcast.4, bf16[1,1024]{1,0:T(2,128)(2,1)} %bitcast.5, s32[4,4]{1,0:T(4,128)} %refs_2_.1, f32[1]{0:T(128)S(6)} %copy.6.refs_3_), custom_call_target="tpu_custom_call" | custom-call | tf_op jit(solution)/shard_map/pallas_call | solution.py:249
  12.6 0.6 %copy.7 = f32[1024,1]{0,1:T(1,128)} copy(f32[1024,1]{0,1:T(1,128)S(1)} %bitcast.3) | data formatting | bytes 8192

commit v6 on v5

--- a/solution.py
+++ b/solution.py
@@ -13,6 +13,7 @@
 WIDE = 2.0**64
 TJ, TI, LAG = 512, 512, 1
 HALVES = ((0, 512), (512, 512))
+KEPT = 256
 
 
 def split3(s):
@@ -36,7 +37,7 @@
     return jnp.concatenate([xt[:80], tail.astype(jnp.bfloat16)], axis=0)
 
 
-def body(x_hbm, v_hbm, m_hbm, h_ref, o_ref, xb, rb, vb, mb, wb, fb, load_sem, sent_x, sent_r, sent_v, got_x, got_r, got_v, note, peer):
+def body(x_hbm, v_hbm, m_hbm, h_ref, o_ref, xb, rb, vb, mb, wb, fb, wp, fp, part_out, part_in, load_sem, sent_x, sent_r, sent_v, sent_t, sent_p, got_x, got_r, got_v, got_p, note, peer):
     y, t, dp = lax.axis_index("rep"), lax.axis_index("team"), lax.axis_index("dp")
     x, c = t // 2, t % 2
     dx = c + y - 2 * c * y
@@ -65,8 +66,8 @@
 
     pl.when(first_chip == 1)(load)
 
-    def copy_x(src, dst, slot, k, d):
-        return pltpu.make_async_remote_copy(src_ref=src, dst_ref=dst, send_sem=sent_x, recv_sem=got_x.at[slot - 1, k], device_id=d, device_id_type=MESH)
+    def copy_x(src, dst, slot, k, d, sent=sent_x):
+        return pltpu.make_async_remote_copy(src_ref=src, dst_ref=dst, send_sem=sent, recv_sem=got_x.at[slot - 1, k], device_id=d, device_id_type=MESH)
 
     def copy_v(src, slot, d):
         return pltpu.make_async_remote_copy(src_ref=src, dst_ref=vb.at[slot], send_sem=sent_v, recv_sem=got_v.at[slot - 1], device_id=d, device_id_type=MESH)
@@ -74,29 +75,29 @@
     def copy_r(src, slot, d):
         return pltpu.make_async_remote_copy(src_ref=src, dst_ref=rb.at[slot], send_sem=sent_r, recv_sem=got_r.at[slot - 1], device_id=d, device_id_type=MESH)
 
-    def send(x_src, r_src, v_src, slot, k, d):
-        cols = pl.ds(*HALVES[k])
+    def send(x_src, r_src, v_src, slot, k, d, at=None, sent=sent_x):
+        cols = pl.ds(*(at or HALVES[k]))
         if k == 0:
             copy_r(r_src, slot, d).start()
-        copy_x(x_src.at[:, cols], xb.at[slot, :, cols], slot, k, d).start()
+        copy_x(x_src.at[:, cols], xb.at[slot, :, cols], slot, k, d, sent).start()
         if k == 0:
             copy_v(v_src, slot, d).start()
 
-    def pass_on(slot, to, k, d):
-        send(xb.at[slot], rb.at[slot], vb.at[slot], to, k, d)
-
-    def arrive(slot, k, name):
+    def pass_on(slot, to, k, d, at=None, sent=sent_x):
+        send(xb.at[slot], rb.at[slot], vb.at[slot], to, k, d, at, sent)
+
+    def arrive(slot, k, name, at=None):
         with jax.named_scope(f"{name}{k}"):
             if k == 0:
                 copy_v(vb.at[slot], slot, partner).wait_recv()
                 copy_r(rb.at[slot], slot, partner).wait_recv()
-            ref = xb.at[slot, :, pl.ds(*HALVES[k])]
+            ref = xb.at[slot, :, pl.ds(*(at or HALVES[k]))]
             copy_x(ref, ref, slot, k, partner).wait_recv()
 
     scale = jnp.where(h_ref[0] > WIDE, 1.0 / WIDE, 1.0)
     alpha = -LOG2E / (h_ref[0] * scale)
 
-    def tiles(*parts):
+    def tiles(*parts, weights=wb, sums=fb):
         total, pend = {}, []
 
         def drain():
@@ -109,17 +110,18 @@
             for slot, team, at in parts:
                 lhs = augment(xb[slot, :, at[0]:at[0] + at[1]], rb[slot, :, at[0]:at[0] + at[1]]).T
                 for j in range(0, at[1], TJ):
-                    rows = lax.broadcasted_iota(jnp.int32, (16, TJ), 0)
-                    v32 = vb[slot, :, at[0] + j:at[0] + j + TJ].astype(jnp.float32)
-                    vv = jnp.where(rows == team, jnp.broadcast_to(v32, (16, TJ)), 0.0).astype(jnp.bfloat16)
+                    size = min(TJ, at[1] - j)
+                    rows = lax.broadcasted_iota(jnp.int32, (16, size), 0)
+                    v32 = vb[slot, :, at[0] + j:at[0] + j + size].astype(jnp.float32)
+                    vv = jnp.where(rows == team, jnp.broadcast_to(v32, (16, size)), 0.0).astype(jnp.bfloat16)
                     for i in range(0, N, TI):
-                        pend.append((i, vv, jnp.dot(lhs[j:j + TJ], wb[:, i:i + TI], preferred_element_type=jnp.float32)))
+                        pend.append((i, vv, jnp.dot(lhs[j:j + size], weights[:, i:i + TI], preferred_element_type=jnp.float32)))
                         if len(pend) > LAG:
                             drain()
             while pend:
                 drain()
             for i in total:
-                fb[:, i:i + TI] += total[i]
+                sums[:, i:i + TI] += total[i]
 
     def prepare():
         fb[...] = jnp.zeros_like(fb)
@@ -178,7 +180,18 @@
 
     pl.when(first_chip == 0)(own_sum)
     tiles((4, team_of(0, 1), (0, N)))
-    weight = jnp.sum(jnp.where(lax.broadcasted_iota(jnp.int32, (4, 4), 1) == t, mb[...].astype(jnp.float32), 0.0), axis=1, keepdims=True)
+    def weight_of(team):
+        mine = lax.broadcasted_iota(jnp.int32, (4, 4), 1) == team
+        return jnp.sum(jnp.where(mine, mb[...].astype(jnp.float32), 0.0), axis=1, keepdims=True)
+
+    weight = weight_of(t)
+
+    @pl.when(dx == 1)
+    def _():
+        fp[...] = jnp.zeros_like(fp)
+        for i in range(0, N, 256):
+            wp[:, i:i + 256] = augment(xb[4, :, i:i + 256], rb[4, :, i:i + 256], scale)
+
 
     f1, f2, p1, p2 = 5 - 3 * dx, 1 + 5 * dx, 6 - 5 * dx, 2 + 3 * dx
 
@@ -193,11 +206,6 @@
         pass_on(f2, 5 - 3 * dx, k, partner)
         return f2, team_of(1 - dx, dx), HALVES[k]
 
-    def third(k):
-        arrive(7, k, "d7_")
-        pass_on(7, 3, k, partner)
-        return 7, team_of(1, 1), HALVES[k]
-
     def first_behind(k):
         arrive(p1, k, "p1_")
         return p1, team_of(dx, 1 - dx), HALVES[k]
@@ -206,32 +214,72 @@
         arrive(p2, k, "p2_")
         return p2, team_of(dx, dx), HALVES[k]
 
-    def third_behind(k):
-        arrive(3, k, "d3_")
-        return 3, team_of(1, 0), HALVES[k]
-
-    ahead = [(got, k) for got in (first, second, third) for k in range(2)]
-    behind = [(got, k) for got in (first_behind, second_behind, third_behind) for k in range(2)]
-    for g in range(7):
-        group = ahead[g:g + 1] + (behind[g - 1:g] if g else [])
-        tiles(*[got(k) for got, k in group])
-
-    o_ref[...] = jnp.sum(fb[0:4] * weight, axis=0, keepdims=True)
+    direct, behind = (7, team_of(1, 1)), (3, team_of(1, 0))
+    cut = (HALVES[1][0], HALVES[1][1] - KEPT)
+    kept = (N - KEPT, KEPT)
+    partial = pltpu.make_async_remote_copy(src_ref=part_out, dst_ref=part_in, send_sem=sent_p, recv_sem=got_p, device_id=partner, device_id_type=MESH)
+
+    def third(k, at=None):
+        arrive(7, k, "d7_")
+        pass_on(7, 3, k, partner, at, sent_t)
+
+    tiles(first(0))
+    tiles(first(1), first_behind(0))
+    tiles(second(0), first_behind(1))
+    tiles(second(1), second_behind(0))
+    third(0)
+    tiles((*direct, HALVES[0]), second_behind(1))
+
+    @pl.when(dx == 0)
+    def _():
+        third(1)
+        arrive(3, 0, "d3_")
+        tiles((*direct, HALVES[1]), (*behind, HALVES[0]))
+        arrive(3, 1, "d3_", cut)
+        tiles((*behind, cut))
+        partial.wait_recv()
+        o_ref[...] = jnp.sum(fb[0:4] * weight, axis=0, keepdims=True) + part_in[...]
+
+    @pl.when(dx == 1)
+    def _():
+        third(1, cut)
+        tiles((*direct, kept), weights=wp, sums=fp)
+        part_out[...] = jnp.sum(fp[0:4] * weight_of(team_of(0, 1)), axis=0, keepdims=True)
+        arrive(3, 0, "d3_")
+        partial.start()
+        tiles((*direct, HALVES[1]), (*behind, HALVES[0]))
+        arrive(3, 1, "d3_")
+        tiles((*behind, HALVES[1]))
+        o_ref[...] = jnp.sum(fb[0:4] * weight, axis=0, keepdims=True)
+
     with jax.named_scope("sendw"):
-        copy_x(xb.at[0:7], xb.at[1:8], 1, 0, partner).wait_send()
+        copy_x(xb.at[0:6], xb.at[1:7], 1, 0, partner).wait_send()
         pltpu.make_async_remote_copy(src_ref=rb.at[0:7], dst_ref=rb.at[1:8], send_sem=sent_r, recv_sem=got_r.at[0], device_id=partner, device_id_type=MESH).wait_send()
         copy = pltpu.make_async_remote_copy(src_ref=vb.at[0:7], dst_ref=vb.at[1:8], send_sem=sent_v, recv_sem=got_v.at[0], device_id=partner, device_id_type=MESH)
         copy.wait_send()
 
+        @pl.when(dx == 0)
+        def _():
+            copy_x(xb.at[7], xb.at[3], 3, 0, partner, sent_t).wait_send()
+
+        @pl.when(dx == 1)
+        def _():
+            ref = xb.at[7, :, 0:N - KEPT]
+            copy_x(ref, ref, 3, 0, partner, sent_t).wait_send()
+            partial.wait_send()
+
 
 SEMS = [
     pltpu.SemaphoreType.DMA((4,)),
+    pltpu.SemaphoreType.DMA,
+    pltpu.SemaphoreType.DMA,
     pltpu.SemaphoreType.DMA,
     pltpu.SemaphoreType.DMA,
     pltpu.SemaphoreType.DMA,
     pltpu.SemaphoreType.DMA((7, 2)),
     pltpu.SemaphoreType.DMA((7,)),
     pltpu.SemaphoreType.DMA((7,)),
+    pltpu.SemaphoreType.DMA,
     pltpu.SemaphoreType.REGULAR,
     pltpu.SemaphoreType.REGULAR,
 ]
@@ -258,6 +306,10 @@
                 pltpu.VMEM((4, 4), jnp.int32),
                 pltpu.VMEM((96, N), jnp.bfloat16),
                 pltpu.VMEM((16, N), jnp.float32),
+                pltpu.VMEM((96, N), jnp.bfloat16),
+                pltpu.VMEM((16, N), jnp.float32),
+                pltpu.VMEM((1, N), jnp.float32),
+                pltpu.VMEM((1, N), jnp.float32),
             ],
             compiler_params=pltpu.CompilerParams(collective_id=0, has_side_effects=True, vmem_limit_bytes=16 * 2**20),
         )(*hbm, bandwidth)

time: 13.3 us -> 13.3 us (level)
  no operation moved by 1% of the time
where the time goes in v6:
time: 13.3 us; the launch traced here: 13.1 us
  Pallas kernels  11.9 us (89%)
  between operations  0.66 us (5%)
  local copies, waits for them, and re-layouts  0.6 us (5%)
    pallas_call x1, Pallas kernels, per_device(): pl.pallas_call(kernel, out_shape=jax.ShapeDtypeStruct((1, N), jnp.float32...  11.9 us
    unnamed x1, local copies, waits for them, and re-layouts  0.6 us

profile of v6, /device:TPU:0, one launch (start us, length us, event | category | flops | bytes accessed | tf_op | source)
XLA Modules:
  0.0 13.1 jit_solution(15044854559829523650)
XLA Ops:
  0.7 11.9 %shard_map.46 = f32[1,1024]{1,0:T(1,128)S(1)} custom-call(bf16[90,1024]{1,0:T(8,128)(2,1)} %bitcast.4, bf16[1,1024]{1,0:T(2,128)(2,1)} %bitcast.5, s32[4,4]{1,0:T(4,128)} %refs_2_.1, f32[1]{0:T(128)S(6)} %copy.6.refs_3_), custom_call_target="tpu_custom_call" | custom-call | tf_op jit(solution)/shard_map/pallas_call | solution.py:297
  12.5 0.6 %copy.7 = f32[1024,1]{0,1:T(1,128)} copy(f32[1024,1]{0,1:T(1,128)S(1)} %bitcast.3) | data formatting | bytes 8192

commit v7 on v6

--- a/solution.py
+++ b/solution.py
@@ -226,12 +226,15 @@
     tiles(first(0))
     tiles(first(1), first_behind(0))
     tiles(second(0), first_behind(1))
-    tiles(second(1), second_behind(0))
-    third(0)
-    tiles((*direct, HALVES[0]), second_behind(1))
+
+    def lead():
+        tiles(second(1), second_behind(0))
+        third(0)
+        tiles((*direct, HALVES[0]), second_behind(1))
 
     @pl.when(dx == 0)
     def _():
+        lead()
         third(1)
         arrive(3, 0, "d3_")
         tiles((*direct, HALVES[1]), (*behind, HALVES[0]))
@@ -242,6 +245,7 @@
 
     @pl.when(dx == 1)
     def _():
+        lead()
         third(1, cut)
         tiles((*direct, kept), weights=wp, sums=fp)
         part_out[...] = jnp.sum(fp[0:4] * weight_of(team_of(0, 1)), axis=0, keepdims=True)

time: 13.3 us -> 13.2 us (level)
  no operation moved by 1% of the time
where the time goes in v7:
time: 13.2 us; the launch traced here: 13.1 us
  Pallas kernels  11.8 us (89%)
  between operations  0.66 us (5%)
  local copies, waits for them, and re-layouts  0.6 us (5%)
    pallas_call x1, Pallas kernels, per_device(): pl.pallas_call(kernel, out_shape=jax.ShapeDtypeStruct((1, N), jnp.float32...  11.8 us
    unnamed x1, local copies, waits for them, and re-layouts  0.6 us

profile of v7, /device:TPU:0, one launch (start us, length us, event | category | flops | bytes accessed | tf_op | source)
XLA Modules:
  0.0 13.1 jit_solution(750045787951229228)
XLA Ops:
  0.7 11.8 %shard_map.46 = f32[1,1024]{1,0:T(1,128)S(1)} custom-call(bf16[90,1024]{1,0:T(8,128)(2,1)} %bitcast.4, bf16[1,1024]{1,0:T(2,128)(2,1)} %bitcast.5, s32[4,4]{1,0:T(4,128)} %refs_2_.1, f32[1]{0:T(128)S(6)} %copy.6.refs_3_), custom_call_target="tpu_custom_call" | custom-call | tf_op jit(solution)/shard_map/pallas_call | solution.py:301
  12.5 0.6 %copy.7 = f32[1024,1]{0,1:T(1,128)} copy(f32[1024,1]{0,1:T(1,128)S(1)} %bitcast.3) | data formatting | bytes 8192
